TPU v7x, 32 devices: a whole 2x2x4 slice. The times are simulated.
32 devices in a mesh: stn: 4 (over z), chan: 4 (over y, core), tile: 2 (over x).
Axes of the slice: x: 2, y: 2, z: 4, core: 2. Of those that a mesh axis runs over, the one named last changes fastest.
Arguments:
- model_image: bfloat16 [8, 64, 2048], P('tile', 'stn'), may hold values from -0.005859375 to 0.005859375
- station_beams: float32 [2, 64, 1024], replicated, may hold values from -6 to 6
- subgrid_offsets: int32 [4, 128, 2], P('chan'), may hold values from -4096 to 4064
- subgrid_stations: int32 [128, 2], P(('stn', 'tile')), may hold values from 0 to 63, as said below
- visibility_uv: float32 [2, 128, 512], P(None, ('stn', 'tile'), 'chan'), may hold values from 2 to 30
- observed: float32 [2, 32, 4, 512], P(None, ('stn', 'tile'), 'chan'), may hold values from -3 to 3
- live_counts: int32 [32, 4], P(('stn', 'tile'), 'chan'), may hold values from 1 to 8
Outputs:
- residual: float32 [2, 32, 4, 512], P(None, ('stn', 'tile'), 'chan')
Inputs may be any that keep to these rules, and one draw needn't show every extreme that they name: `subgrid_stations`: each row names two different stations. `live_counts`: rows with a time step at or beyond the count carry no data.
All inputs are finite; a program needn't handle non-finite values.
Results may differ from a plain program's by a relative error of at most 0.00071.
Values may be sent and summed in bfloat16 or wider, within the bound.
A program may use at most 64 MiB of HBM per device.

v0:
```python
import math
import jax
import jax.numpy as jnp
from jax import lax
from jax.sharding import PartitionSpec as P

SG = 32
NG = 8192
TIMES = 8
TILE_DEV = 4
TL = 64
SUB_TILE = 16
two_pi = 6.283185307179586


def phase_pair(products, modulus):
    angle_turns = jnp.mod(products, modulus).astype(jnp.float32) * (two_pi / modulus)
    return (jnp.cos(angle_turns), -jnp.sin(angle_turns))


def narrow_mix(pattern, left, right):
    return jnp.einsum(pattern, left, right, preferred_element_type=jnp.float32)


def exact_mix(pattern, left, right):
    return jnp.einsum(pattern, left, right, precision=lax.Precision.HIGHEST)


def tile_cuts(strip_rows, row_ids, offset_block, strip_half):
    block_size = offset_block.shape[0]
    columns = strip_rows.shape[1]
    pixel_idx = jnp.arange(SG, dtype=jnp.int32)
    col_pos = jnp.arange(columns, dtype=jnp.int32) - columns // 2
    v_index = offset_block[:, 1][:, None] + pixel_idx[None, :]
    ev_real, ev_imag = phase_pair(col_pos[:, None, None] * v_index[None, :, :], NG)
    phase_table = (
        jnp.stack([ev_real, ev_imag], axis=1)
        .reshape(columns, 2 * block_size * SG)
        .astype(jnp.bfloat16)
    )
    partial_q = jnp.dot(strip_rows, phase_table, preferred_element_type=jnp.float32).astype(
        jnp.bfloat16
    )
    partial_q = partial_q.reshape(strip_rows.shape[0], 2, block_size, SG)
    q_real = partial_q[:, 0]
    q_imag = partial_q[:, 1]
    u_index = offset_block[:, 0][:, None] + pixel_idx[None, :]
    row_pos = row_ids - strip_half
    eu_real, eu_imag = phase_pair(u_index[:, :, None] * row_pos[None, None, :], NG)
    eu_real = eu_real.astype(jnp.bfloat16)
    eu_imag = eu_imag.astype(jnp.bfloat16)
    cut_real = narrow_mix("jal,ljb->jab", eu_real, q_real) - narrow_mix(
        "jal,ljb->jab", eu_imag, q_imag
    )
    cut_imag = narrow_mix("jal,ljb->jab", eu_real, q_imag) + narrow_mix(
        "jal,ljb->jab", eu_imag, q_real
    )
    return jnp.stack([cut_real, cut_imag], axis=1).reshape(block_size, 2 * SG * SG)


def cuts_blocked(strip_rows, row_ids, offsets, strip_half):
    how_many = offsets.shape[0]
    block_size = math.gcd(how_many, 32)
    grouped = offsets.reshape(how_many // block_size, block_size, 2)
    stacked = lax.map(
        lambda offset_block: tile_cuts(strip_rows, row_ids, offset_block, strip_half), grouped
    )
    return stacked.reshape(how_many, 2 * SG * SG)


def predict(cut_rows, pair_ids, station_beams, uv_block):
    how_many = cut_rows.shape[0]
    cut_grid = cut_rows.reshape(how_many, 2, SG, SG)
    pixel_idx = jnp.arange(SG, dtype=jnp.int32)
    w_real, w_neg = phase_pair(pixel_idx[:, None] * pixel_idx[None, :], SG)
    w_imag = -w_neg
    c_real = cut_grid[:, 0]
    c_imag = cut_grid[:, 1]
    half_real = exact_mix("xa,jab->jxb", w_real, c_real) - exact_mix("xa,jab->jxb", w_imag, c_imag)
    half_imag = exact_mix("xa,jab->jxb", w_real, c_imag) + exact_mix("xa,jab->jxb", w_imag, c_real)
    sub_real = (
        exact_mix("jxb,yb->jxy", half_real, w_real) - exact_mix("jxb,yb->jxy", half_imag, w_imag)
    ) / (SG * SG)
    sub_imag = (
        exact_mix("jxb,yb->jxy", half_real, w_imag) + exact_mix("jxb,yb->jxy", half_imag, w_real)
    ) / (SG * SG)
    pixel_pos = pixel_idx.astype(jnp.float32)
    taper_line = 1.0 - ((2.0 * pixel_pos - (SG - 1)) / SG) ** 2
    taper_grid = (taper_line[:, None] * taper_line[None, :]).reshape(SG * SG)
    beam_first = station_beams[:, pair_ids[:, 0]]
    beam_second = station_beams[:, pair_ids[:, 1]]
    gain_real = (beam_first[0] * beam_second[0] + beam_first[1] * beam_second[1]) * taper_grid
    gain_imag = (beam_first[1] * beam_second[0] - beam_first[0] * beam_second[1]) * taper_grid
    flat_real = sub_real.reshape(how_many, SG * SG)
    flat_imag = sub_imag.reshape(how_many, SG * SG)
    weighted_real = (flat_real * gain_real - flat_imag * gain_imag).reshape(how_many, SG, SG)
    weighted_imag = (flat_real * gain_imag + flat_imag * gain_real).reshape(how_many, SG, SG)
    u_angle = uv_block[0][:, :, None] * pixel_pos[None, None, :] * (two_pi / SG)
    v_angle = uv_block[1][:, :, None] * pixel_pos[None, None, :] * (two_pi / SG)
    eu_real = jnp.cos(u_angle)
    eu_imag = -jnp.sin(u_angle)
    ev_real = jnp.cos(v_angle)
    ev_imag = -jnp.sin(v_angle)
    inner_real = exact_mix("jxy,jky->jxk", weighted_real, ev_real) - exact_mix(
        "jxy,jky->jxk", weighted_imag, ev_imag
    )
    inner_imag = exact_mix("jxy,jky->jxk", weighted_real, ev_imag) + exact_mix(
        "jxy,jky->jxk", weighted_imag, ev_real
    )
    vis_real = exact_mix("jkx,jxk->jk", eu_real, inner_real) - exact_mix(
        "jkx,jxk->jk", eu_imag, inner_imag
    )
    vis_imag = exact_mix("jkx,jxk->jk", eu_real, inner_imag) + exact_mix(
        "jkx,jxk->jk", eu_imag, inner_real
    )
    return jnp.stack([vis_real, vis_imag], axis=0)


def on_device(
    model_image,
    station_beams,
    subgrid_offsets,
    subgrid_stations,
    visibility_uv,
    observed,
    live_counts,
):
    tile_count = lax.axis_size("tile")
    columns = model_image.shape[2]
    strip_half = TILE_DEV * tile_count * TL // 2
    group_offsets = subgrid_offsets[0]
    stn_index = lax.axis_index("stn")
    tile_first = lax.axis_index("tile") * TILE_DEV
    tile_ids = jnp.arange(TILE_DEV, dtype=jnp.int32)
    group_size = SUB_TILE * tile_count
    station_offsets = lax.dynamic_slice_in_dim(group_offsets, stn_index * group_size, group_size, 0)
    shard_piece = lax.all_gather(model_image, "stn", axis=1, tiled=True)
    piece_rows = shard_piece.shape[1]
    piece_ids = (
        (tile_first + tile_ids)[:, None] * TL + jnp.arange(piece_rows, dtype=jnp.int32)[None, :]
    ).reshape(-1)
    piece_strip = shard_piece.reshape(TILE_DEV * piece_rows, columns)
    group_cuts = cuts_blocked(piece_strip, piece_ids, station_offsets, strip_half)
    own_cuts = lax.psum_scatter(group_cuts, "tile", scatter_dimension=0, tiled=True)
    predicted = predict(own_cuts, subgrid_stations, station_beams, visibility_uv)
    chan_count = lax.axis_size("chan")
    outgoing = predicted.reshape(2, SUB_TILE // chan_count, chan_count, predicted.shape[2])
    regrouped = lax.all_to_all(outgoing, "chan", split_axis=2, concat_axis=3, tiled=True)
    total_rows = regrouped.shape[3]
    time_step = jnp.mod(jnp.arange(total_rows, dtype=jnp.int32), TIMES)
    live_mask = time_step[None, None, :] < live_counts[:, :, None]
    return jnp.where(live_mask[None], observed - regrouped, 0.0)


def solution(mesh):
    return jax.shard_map(
        on_device,
        mesh=mesh,
        in_specs=(
            P("tile", "stn", None),
            P(),
            P("chan", None, None),
            P(("stn", "tile"), None),
            P(None, ("stn", "tile"), "chan"),
            P(None, ("stn", "tile"), "chan", None),
            P(("stn", "tile"), "chan"),
        ),
        out_specs=P(None, ("stn", "tile"), "chan", None),
        check_vma=False,
    )
```

profile of v0, /device:TPU:0, one launch (start us, length us, event | category | flops | bytes accessed | tf_op | source)
XLA Modules:
  0.0 118.8 jit_solution(3581766435553474679)
XLA Ops:
  6.5 0.7 all-gather.2.cloned.1.call-update
  7.3 0.8 dynamic-slice_bitcast_fusion
  8.3 0.8 fusion.66
  9.1 0.7 gather_fusion
  9.9 0.7 gather_fusion.1
  11.0 35.5 %cosine_convert_fusion = (bf16[2048,1,32,32]{0,3,2,1:T(8,128)(2,1)S(1)}, bf16[2048,1,32,32]{0,3,2,1:T(8,128)(2,1)}) fusion(s32[32,32]{1,0:T(8,128)S(1)} %iota_add_fusion, s32[2048]{0:T(1024)S(1)} %iota_add_fusion.2), kind=kLoop, calls=%fused_computation.12 | loop fusion | flops 35651584 | bytes 8400896 | tf_op jit(solution)/shard_map/convert
  46.4 6.2 %pad_maximum_fusion = bf16[2048,2,32,32]{0,3,2,1:T(8,128)(2,1)} fusion(bf16[2048,1,32,32]{0,3,2,1:T(8,128)(2,1)} %get-tuple-element.31, bf16[2048,1,32,32]{0,3,2,1:T(8,128)(2,1)S(1)} %get-tuple-element.30), kind=kLoop, calls=%fused_computation.10 | loop fusion | flops 4194304 | bytes 16777216 | tf_op jit(solution)/shard_map/while/body/eval_jaxpr/stack | solution.py:37
  52.6 6.0 %convolution_convert_fusion = bf16[2048,256]{1,0:T(8,128)(2,1)S(1)} fusion(bf16[2048,2048]{0,1:T(8,128)(2,1)} %bitcast.90, bf16[256,2048]{1,0:T(8,128)(2,1)} %bitcast.96), kind=kOutput, calls=%fused_computation.13 | convolution fusion | flops 2148007936 | bytes 10485760 | tf_op jit(solution)/shard_map/while/body/eval_jaxpr/dot_general | solution.py:41
  58.6 4.0 %fusion.15 = f32[32,32,32]{2,1,0:T(8,128)S(1)} fusion(s32[256]{0:T(256)S(1)} %sub.67, s32[32,32]{1,0:T(8,128)S(1)} %iota_add_fusion.1, bf16[256,2,32,32]{0,3,2,1:T(8,128)(2,1)S(1)} %bitcast.97), kind=kOutput, calls=%fused_computation.44 | convolution fusion | flops 20709376 | bytes 672768 | tf_op jit(solution)/shard_map/while/body/eval_jaxpr/jal,ljb->jab/dot_general | solution.py:22
  62.6 4.0 %fusion.14 = f32[32,32,32]{2,1,0:T(8,128)S(1)} fusion(s32[256]{0:T(256)S(1)} %sub.67, s32[32,32]{1,0:T(8,128)S(1)} %iota_add_fusion.1, bf16[256,2,32,32]{0,3,2,1:T(8,128)(2,1)S(1)} %bitcast.98), kind=kOutput, calls=%fused_computation.43 | convolution fusion | flops 20709376 | bytes 672768 | tf_op jit(solution)/shard_map/while/body/eval_jaxpr/jal,ljb->jab/dot_general | solution.py:22
  66.6 4.3 %fusion.4 = f32[32,1,32,32]{3,2,0,1:T(8,128)S(1)} fusion(f32[32,32,32]{2,1,0:T(8,128)S(1)} %fusion.15, s32[256]{0:T(256)S(1)} %sub.67, s32[32,32]{1,0:T(8,128)S(1)} %iota_add_fusion.1, bf16[256,2,32,32]{0,3,2,1:T(8,128)(2,1)S(1)} %bitcast.99), kind=kOutput, calls=%fused_computation.22 | convolution fusion | flops 21004288 | bytes 1197056 | tf_op jit(solution)/shard_map/while/body/eval_jaxpr/jal,ljb->jab/dot_general | solution.py:22
  70.9 4.1 %fusion.3 = f32[32,1,32,32]{3,2,0,1:T(8,128)S(1)} fusion(f32[32,32,32]{2,1,0:T(8,128)S(1)} %fusion.14, s32[256]{0:T(256)S(1)} %sub.67, s32[32,32]{1,0:T(8,128)S(1)} %iota_add_fusion.1, bf16[256,2,32,32]{0,3,2,1:T(8,128)(2,1)S(1)} %bitcast.100), kind=kOutput, calls=%fused_computation.20 | convolution fusion | flops 21004288 | bytes 1197056 | tf_op jit(solution)/shard_map/while/body/eval_jaxpr/jal,ljb->jab/dot_general | solution.py:22
  75.2 1.2 %reshape.278 = f32[32,2048]{1,0:T(8,128)} reshape(f32[32,2,32,32]{3,2,1,0:T(8,128)S(1)} %copy.26) | data formatting | bytes 524288 | tf_op jit(solution)/shard_map/reshape | solution.py:68
  76.5 14.6 %reduce-scatter.2.cloned.1.call-done = f32[16,2048]{1,0:T(8,128)} async-done(((f32[32,2048]{1,0:T(8,128)}), f32[16,2048]{1,0:T(8,128)}) %reduce-scatter.2.cloned.1.call-update) | async-done | bytes 131088 | tf_op jit(solution)/shard_map/reduce_scatter | solution.py:144
  91.1 1.1 reshape.279
  95.8 0.9 fusion.8
  97.2 1.3 %fusion.18 = f32[16,32,128]{2,1,0:T(8,128)S(1)} fusion(f32[16,32,32]{2,1,0:T(8,128)S(1)} %get-tuple-element.27, f32[16,128]{1,0:T(8,128)S(1)} %get-tuple-element.33, f32[32]{0:T(128)S(1)} %iota_convert_fusion), kind=kOutput, calls=%fused_computation.56 | convolution fusion | flops 25296896 | bytes 336000 | tf_op jit(solution)/shard_map/jxy,jky->jxk/dot_general | solution.py:26
  98.6 1.3 %fusion.20 = f32[16,32,128]{2,1,0:T(8,128)S(1)} fusion(f32[16,32,32]{2,1,0:T(8,128)S(1)} %get-tuple-element.27, f32[16,128]{1,0:T(8,128)S(1)} %get-tuple-element.33, f32[32]{0:T(128)S(1)} %iota_convert_fusion), kind=kOutput, calls=%fused_computation.57 | convolution fusion | flops 25362432 | bytes 336000 | tf_op jit(solution)/shard_map/jxy,jky->jxk/dot_general | solution.py:26
  99.9 1.3 %fusion.6 = f32[16,128,32]{1,2,0:T(8,128)S(1)} fusion(f32[16,32,128]{2,1,0:T(8,128)S(1)} %fusion.18, f32[16,32,32]{2,1,0:T(8,128)S(1)} %get-tuple-element.26, f32[16,128]{1,0:T(8,128)S(1)} %get-tuple-element.33, f32[32]{0:T(128)S(1)} %iota_convert_fusion), kind=kOutput, calls=%fused_computation.26 | convolution fusion | flops 25427968 | bytes 598144 | tf_op jit(solution)/shard_map/jxy,jky->jxk/dot_general | solution.py:26
  101.2 2.4 %multiply_reduce_fusion.2 = (f32[16,128]{1,0:T(8,128)S(1)}, f32[16,128]{1,0:T(8,128)S(1)}, f32[16,128]{1,0:T(8,128)S(1)}, f32[16,128]{1,0:T(8,128)S(1)}) fusion(f32[32]{0:T(128)S(1)} %iota_convert_fusion, f32[16,128]{1,0:T(8,128)S(1)} %get-tuple-element.32, f32[16,128,32]{1,2,0:T(8,128)S(1)} %fusion.6, f32[16,32,128]{2,1,0:T(8,128)S(1)} %fusion.20, ...), kind=kOutput, calls=%fused_computation.49 | convolution fusion | flops 26075136 | bytes 639104 | tf_op jit(solution)/shard_map/jxy,jky->jxk/dot_general | solution.py:26
  103.6 0.6 copy.33
  104.2 3.3 %all-to-all-start = ((f32[2,4,4,128]{3,1,0,2:T(4,128)}), f32[2,4,4,128]{3,1,0,2:T(4,128)S(1)}, u32[]{:S(2)}, u32[]{:S(2)}) async-start(f32[2,4,4,128]{3,1,0,2:T(4,128)} %copy.33), calls=%async_computation.1 | async-start | bytes 32768 | tf_op jit(solution)/shard_map/all_to_all | solution.py:148
  107.6 3.7 %all-to-all-done = f32[2,4,4,128]{3,1,0,2:T(4,128)S(1)} async-done(((f32[2,4,4,128]{3,1,0,2:T(4,128)}), f32[2,4,4,128]{3,1,0,2:T(4,128)S(1)}, u32[]{:S(2)}, u32[]{:S(2)}) %all-to-all-start) | async-done | bytes 16416 | tf_op jit(solution)/shard_map/all_to_all | solution.py:148
  111.4 0.6 copy.36
  (44 shorter events, 5.2 us)
Async XLA Ops:
  6.5 2.6 %copy-start = (f32[2,64,1024]{2,1,0:T(8,128)S(1)}, f32[2,64,1024]{2,1,0:T(8,128)}, u32[]{:S(2)}) copy-start(f32[2,64,1024]{2,1,0:T(8,128)} %param.8) | copy-start | bytes 1572868
  6.5 46.1 %all-gather.2.cloned.1.call-start = ((), (), s32[]{:S(2)}) async-start(), calls=%async_computation.2 | async-start | bytes 1310720 | tf_op jit(solution)/shard_map/all_gather | solution.py:137
  7.3 83.8 %reduce-scatter.2.cloned.1.call-start = ((), (), s32[]{:S(2)}) async-start(), calls=%async_computation.3 | async-start | bytes 393216 | tf_op jit(solution)/shard_map/reduce_scatter | solution.py:144
  66.6 9.9 %copy-start.2 = (f32[2,16,128]{2,1,0:T(8,128)S(1)}, f32[2,16,128]{2,1,0:T(8,128)}, u32[]{:S(2)}) copy-start(f32[2,16,128]{2,1,0:T(8,128)} %param.11) | copy-start | bytes 49156
  75.0 32.5 %copy-start.3 = (s32[4,1]{0,1:T(1,128)S(1)}, s32[4,1]{0,1:T(1,128)}, u32[]{:S(2)}) copy-start(s32[4,1]{0,1:T(1,128)} %param.13) | copy-start | bytes 52
  75.0 36.3 %copy-start.1 = (f32[2,4,1,512]{3,2,1,0:T(1,128)S(1)}, f32[2,4,1,512]{3,2,1,0:T(1,128)}, u32[]{:S(2)}) copy-start(f32[2,4,1,512]{3,2,1,0:T(1,128)} %param.12) | copy-start | bytes 49156
  104.2 7.1 %all-to-all-start = ((f32[2,4,4,128]{3,1,0,2:T(4,128)}), f32[2,4,4,128]{3,1,0,2:T(4,128)S(1)}, u32[]{:S(2)}, u32[]{:S(2)}) async-start(f32[2,4,4,128]{3,1,0,2:T(4,128)} %copy.33), calls=%async_computation.1 | async-start | bytes 32768 | tf_op jit(solution)/shard_map/all_to_all | solution.py:148
Sparse Core Ops, SparseCore 0:
  8.9 30.7 all-gather.1
  76.6 14.4 reduce-scatter.1
where the time goes:
time: 119 us
  other arithmetic  43 us (36%)
  matrix products  33.7 us (28%)
  waiting for transfers between devices  19 us (16%)
  between operations  13.6 us (11%)
  local copies, waits for them, and re-layouts  6.18 us (5%)
  starting transfers between devices  3.3 us (3%)
    another operation x1, other arithmetic  35.5 us
    dot_general x4, matrix products, narrow_mix(): return jnp.einsum(pattern, left, right, preferred_element_type=jnp.float32)  16.4 us
    reduce_scatter x1, waiting for transfers between devices, on_device(): lax.psum_scatter(group_cuts, 'tile', scatter_dimension=0, tiled=True)  14.6 us
    dot_general x12, matrix products, exact_mix(): return jnp.einsum(pattern, left, right, precision=lax.Precision.HIGHEST)  11.3 us
    another operation x1, other arithmetic, tile_cuts(): jnp.stack([ev_real, ev_imag], axis=1).reshape(columns, 2 * block_size * SG)  6.18 us
    dot_general x1, matrix products, tile_cuts(): jnp.dot(strip_rows, phase_table, preferred_element_type=jnp.float32)  6 us
    all_to_all x1, waiting for transfers between devices, on_device(): lax.all_to_all(outgoing, 'chan', split_axis=2, concat_axis=3, tiled=True)  3.74 us
    all_to_all x1, starting transfers between devices, on_device(): lax.all_to_all(outgoing, 'chan', split_axis=2, concat_axis=3, tiled=True)  3.25 us
  transfers between devices with their start and end apart: 3, of which 2 were waited for; matrix products, arithmetic and copies ran while one was open for 38% of the time, Pallas kernels for 0%

commit v1 on v0

--- a/solution.py
+++ b/solution.py
@@ -11,6 +11,17 @@
 TL = 64
 SUB_TILE = 16
 two_pi = 6.283185307179586
+
+
+def in_blocks(x, dim, size):
+    before, after = (x.shape[:dim], x.shape[dim + 1 :])
+    return jnp.moveaxis(x.reshape(*before, size, -1, *after), dim, 0)
+
+
+def laid_out(blocks, dim):
+    dims = list(blocks.shape[1:])
+    dims[dim] *= blocks.shape[0]
+    return jnp.moveaxis(blocks, 0, dim).reshape(dims)
 
 
 def phase_pair(products, modulus):
@@ -145,7 +156,14 @@
     predicted = predict(own_cuts, subgrid_stations, station_beams, visibility_uv)
     chan_count = lax.axis_size("chan")
     outgoing = predicted.reshape(2, SUB_TILE // chan_count, chan_count, predicted.shape[2])
-    regrouped = lax.all_to_all(outgoing, "chan", split_axis=2, concat_axis=3, tiled=True)
+    peers, index = (lax.axis_size("chan"), lax.axis_index("chan"))
+    blocks = in_blocks(outgoing, 2, peers)
+    done = [blocks[index]]
+    for step in range(1, peers):
+        sent = blocks[(index + step) % peers]
+        done.append(lax.ppermute(sent, "chan", [(i, (i + step) % peers) for i in range(peers)]))
+    blocks = jnp.stack(done)[(index - jnp.arange(peers)) % peers]
+    regrouped = laid_out(blocks, 3)
     total_rows = regrouped.shape[3]
     time_step = jnp.mod(jnp.arange(total_rows, dtype=jnp.int32), TIMES)
     live_mask = time_step[None, None, :] < live_counts[:, :, None]

time: 119 us -> 117 us (0.983)
  waiting for transfers between devices: 19 us -> 16.6 us
  other arithmetic: 43 us -> 44.3 us
    all_to_all x1 -> x0, waiting for transfers between devices: 3.74 us -> none  [on_device(): lax.all_to_all(outgoing, 'chan', split_axis=2, concat_axis=3, tiled=True)]
    all_to_all x1 -> x0, starting transfers between devices: 3.25 us -> none  [on_device(): lax.all_to_all(outgoing, 'chan', split_axis=2, concat_axis=3, tiled=True)]
    ppermute x0 -> x3, starting transfers between devices: none -> 2.96 us  [on_device(): lax.ppermute(sent, 'chan', [(i, (i + step) % peers) for i in range(peers)])]
    ppermute x0 -> x3, waiting for transfers between devices: none -> 1.32 us  [on_device(): lax.ppermute(sent, 'chan', [(i, (i + step) % peers) for i in range(peers)])]
    another operation x1 -> x2, other arithmetic: 35.5 us -> 35.5 us
  transfers between devices with their start and end apart: 3 -> 5, of which waited for: 2 -> 4; matrix products, arithmetic and copies ran while one was open for 38% -> 39% of each run, Pallas kernels for 0% -> 0%
where the time goes in v1:
time: 117 us
  other arithmetic  44.3 us (38%)
  matrix products  33.8 us (29%)
  waiting for transfers between devices  16.6 us (14%)
  between operations  13.7 us (12%)
  local copies, waits for them, and re-layouts  5.5 us (5%)
  starting transfers between devices  3 us (3%)
    another operation x1, other arithmetic  35.5 us
    dot_general x4, matrix products, narrow_mix(): return jnp.einsum(pattern, left, right, preferred_element_type=jnp.float32)  16.4 us
    reduce_scatter x1, waiting for transfers between devices, on_device(): lax.psum_scatter(group_cuts, 'tile', scatter_dimension=0, tiled=True)  14.5 us
    dot_general x12, matrix products, exact_mix(): return jnp.einsum(pattern, left, right, precision=lax.Precision.HIGHEST)  11.4 us
    another operation x1, other arithmetic, tile_cuts(): jnp.stack([ev_real, ev_imag], axis=1).reshape(columns, 2 * block_size * SG)  6.18 us
    dot_general x1, matrix products, tile_cuts(): jnp.dot(strip_rows, phase_table, preferred_element_type=jnp.float32)  6 us
    ppermute x3, starting transfers between devices, on_device(): lax.ppermute(sent, 'chan', [(i, (i + step) % peers) for i in range(peers)])  2.96 us
  transfers between devices with their start and end apart: 5, of which 4 were waited for; matrix products, arithmetic and copies ran while one was open for 39% of the time, Pallas kernels for 0%

profile of v1, /device:TPU:0, one launch (start us, length us, event | category | flops | bytes accessed | tf_op | source)
XLA Modules:
  0.0 116.8 jit_solution(2856119999899609567)
XLA Ops:
  6.5 0.7 all-gather.2.cloned.1.call-update
  7.3 0.8 fusion.81
  8.3 0.8 fusion.83
  9.1 0.7 gather_fusion
  9.9 0.7 gather_fusion.1
  10.6 0.7 broadcast_compare_fusion
  11.7 35.5 %cosine_convert_fusion = (bf16[2048,1,32,32]{0,3,2,1:T(8,128)(2,1)S(1)}, bf16[2048,1,32,32]{0,3,2,1:T(8,128)(2,1)}) fusion(s32[32,32]{1,0:T(8,128)S(1)} %iota_add_fusion, s32[2048]{0:T(1024)S(1)} %iota_add_fusion.2), kind=kLoop, calls=%fused_computation.13 | loop fusion | flops 35651584 | bytes 8400896 | tf_op jit(solution)/shard_map/convert
  47.2 6.2 %pad_maximum_fusion = bf16[2048,2,32,32]{0,3,2,1:T(8,128)(2,1)} fusion(bf16[2048,1,32,32]{0,3,2,1:T(8,128)(2,1)} %get-tuple-element.31, bf16[2048,1,32,32]{0,3,2,1:T(8,128)(2,1)S(1)} %get-tuple-element.30), kind=kLoop, calls=%fused_computation.11 | loop fusion | flops 4194304 | bytes 16777216 | tf_op jit(solution)/shard_map/while/body/eval_jaxpr/stack | solution.py:48
  53.4 6.0 %convolution_convert_fusion = bf16[2048,256]{1,0:T(8,128)(2,1)S(1)} fusion(bf16[2048,2048]{0,1:T(8,128)(2,1)} %bitcast.105, bf16[256,2048]{1,0:T(8,128)(2,1)} %bitcast.120), kind=kOutput, calls=%fused_computation.14 | convolution fusion | flops 2148007936 | bytes 10485760 | tf_op jit(solution)/shard_map/while/body/eval_jaxpr/dot_general | solution.py:52
  59.4 4.0 %fusion.15 = f32[32,32,32]{2,1,0:T(8,128)S(1)} fusion(s32[256]{0:T(256)S(1)} %sub.80, s32[32,32]{1,0:T(8,128)S(1)} %iota_add_fusion.1, bf16[256,2,32,32]{0,3,2,1:T(8,128)(2,1)S(1)} %bitcast.121), kind=kOutput, calls=%fused_computation.45 | convolution fusion | flops 20709376 | bytes 672768 | tf_op jit(solution)/shard_map/while/body/eval_jaxpr/jal,ljb->jab/dot_general | solution.py:33
  63.4 4.0 %fusion.14 = f32[32,32,32]{2,1,0:T(8,128)S(1)} fusion(s32[256]{0:T(256)S(1)} %sub.80, s32[32,32]{1,0:T(8,128)S(1)} %iota_add_fusion.1, bf16[256,2,32,32]{0,3,2,1:T(8,128)(2,1)S(1)} %bitcast.122), kind=kOutput, calls=%fused_computation.44 | convolution fusion | flops 20709376 | bytes 672768 | tf_op jit(solution)/shard_map/while/body/eval_jaxpr/jal,ljb->jab/dot_general | solution.py:33
  67.4 4.3 %fusion.4 = f32[32,1,32,32]{3,2,0,1:T(8,128)S(1)} fusion(f32[32,32,32]{2,1,0:T(8,128)S(1)} %fusion.15, s32[256]{0:T(256)S(1)} %sub.80, s32[32,32]{1,0:T(8,128)S(1)} %iota_add_fusion.1, bf16[256,2,32,32]{0,3,2,1:T(8,128)(2,1)S(1)} %bitcast.123), kind=kOutput, calls=%fused_computation.23 | convolution fusion | flops 21004288 | bytes 1197056 | tf_op jit(solution)/shard_map/while/body/eval_jaxpr/jal,ljb->jab/dot_general | solution.py:33
  71.7 4.1 %fusion.3 = f32[32,1,32,32]{3,2,0,1:T(8,128)S(1)} fusion(f32[32,32,32]{2,1,0:T(8,128)S(1)} %fusion.14, s32[256]{0:T(256)S(1)} %sub.80, s32[32,32]{1,0:T(8,128)S(1)} %iota_add_fusion.1, bf16[256,2,32,32]{0,3,2,1:T(8,128)(2,1)S(1)} %bitcast.124), kind=kOutput, calls=%fused_computation.21 | convolution fusion | flops 21004288 | bytes 1197056 | tf_op jit(solution)/shard_map/while/body/eval_jaxpr/jal,ljb->jab/dot_general | solution.py:33
  76.0 1.2 %reshape.333 = f32[32,2048]{1,0:T(8,128)} reshape(f32[32,2,32,32]{3,2,1,0:T(8,128)S(1)} %copy.19) | data formatting | bytes 524288 | tf_op jit(solution)/shard_map/reshape | solution.py:79
  77.3 14.5 %reduce-scatter.2.cloned.1.call-done = f32[16,2048]{1,0:T(8,128)} async-done(((f32[32,2048]{1,0:T(8,128)}), f32[16,2048]{1,0:T(8,128)}) %reduce-scatter.2.cloned.1.call-update) | async-done | bytes 131088 | tf_op jit(solution)/shard_map/reduce_scatter | solution.py:155
  91.8 1.1 reshape.334
  96.5 0.9 fusion.8
  98.0 1.3 %fusion.20 = f32[16,32,128]{2,1,0:T(8,128)S(1)} fusion(f32[16,32,32]{2,1,0:T(8,128)S(1)} %get-tuple-element.27, f32[16,128]{1,0:T(8,128)S(1)} %get-tuple-element.37, f32[32]{0:T(128)S(1)} %iota_convert_fusion), kind=kOutput, calls=%fused_computation.58 | convolution fusion | flops 25362432 | bytes 336000 | tf_op jit(solution)/shard_map/jxy,jky->jxk/dot_general | solution.py:37
  99.3 1.3 %fusion.18 = f32[16,32,128]{2,1,0:T(8,128)S(1)} fusion(f32[16,32,32]{2,1,0:T(8,128)S(1)} %get-tuple-element.27, f32[16,128]{1,0:T(8,128)S(1)} %get-tuple-element.37, f32[32]{0:T(128)S(1)} %iota_convert_fusion), kind=kOutput, calls=%fused_computation.57 | convolution fusion | flops 25296896 | bytes 336000 | tf_op jit(solution)/shard_map/jxy,jky->jxk/dot_general | solution.py:37
  100.6 1.3 %fusion.5 = f32[16,128,32]{1,2,0:T(8,128)S(1)} fusion(f32[16,32,128]{2,1,0:T(8,128)S(1)} %fusion.20, f32[16,32,32]{2,1,0:T(8,128)S(1)} %get-tuple-element.26, f32[16,128]{1,0:T(8,128)S(1)} %get-tuple-element.37, f32[32]{0:T(128)S(1)} %iota_convert_fusion), kind=kOutput, calls=%fused_computation.25 | convolution fusion | flops 25362432 | bytes 598144 | tf_op jit(solution)/shard_map/jxy,jky->jxk/dot_general | solution.py:37
  102.0 2.4 %multiply_reduce_fusion = (f32[16,128]{1,0:T(8,128)S(1)}, f32[16,128]{1,0:T(8,128)S(1)}, f32[16,128]{1,0:T(8,128)S(1)}, f32[16,128]{1,0:T(8,128)S(1)}) fusion(f32[32]{0:T(128)S(1)} %iota_convert_fusion, f32[16,128]{1,0:T(8,128)S(1)} %get-tuple-element.36, f32[16,128,32]{1,2,0:T(8,128)S(1)} %fusion.5, f32[16,32,128]{2,1,0:T(8,128)S(1)} %fusion.18, ...), kind=kOutput, calls=%fused_computation.48 | convolution fusion | flops 26140672 | bytes 639104 | tf_op jit(solution)/shard_map/jxy,jky->jxk/dot_general | solution.py:37
  104.5 1.5 %collective-permute-start.1 = (f32[2,4,1,128]{3,1,0,2:T(4,128)S(1)}, f32[2,4,1,128]{3,1,0,2:T(4,128)S(1)}, u32[]{:S(2)}, u32[]{:S(2)}) collective-permute-start(f32[2,4,1,128]{3,1,0,2:T(4,128)S(1)} %bitcast.114), channel_id=1, source_target_pairs={{0,4},{2,6},{4,0},{6,2},{1,5},{3,7},{5,1},{7,3},{8,12},{10,14},{12... | collective-permute-start | bytes 12296 | tf_op jit(solution)/shard_map/ppermute | solution.py:164
  106.0 1.4 %collective-permute-start.2 = (f32[2,4,1,128]{3,1,0,2:T(4,128)S(1)}, f32[2,4,1,128]{3,1,0,2:T(4,128)S(1)}, u32[]{:S(2)}, u32[]{:S(2)}) collective-permute-start(f32[2,4,1,128]{3,1,0,2:T(4,128)S(1)} %bitcast.113), channel_id=1, source_target_pairs={{0,6},{2,0},{4,2},{6,4},{1,7},{3,1},{5,3},{7,5},{8,14},{10,8},{12,... | collective-permute-start | bytes 12296 | tf_op jit(solution)/shard_map/ppermute | solution.py:164
  107.5 0.7 collective-permute-done.1
  (47 shorter events, 7.1 us)
Async XLA Ops:
  6.5 2.6 %copy-start = (f32[2,64,1024]{2,1,0:T(8,128)S(1)}, f32[2,64,1024]{2,1,0:T(8,128)}, u32[]{:S(2)}) copy-start(f32[2,64,1024]{2,1,0:T(8,128)} %param.8) | copy-start | bytes 1572868
  6.5 46.8 %all-gather.2.cloned.1.call-start = ((), (), s32[]{:S(2)}) async-start(), calls=%async_computation.1 | async-start | bytes 1310720 | tf_op jit(solution)/shard_map/all_gather | solution.py:148
  7.3 84.6 %reduce-scatter.2.cloned.1.call-start = ((), (), s32[]{:S(2)}) async-start(), calls=%async_computation.2 | async-start | bytes 393216 | tf_op jit(solution)/shard_map/reduce_scatter | solution.py:155
  67.4 9.9 %copy-start.2 = (f32[2,16,128]{2,1,0:T(8,128)S(1)}, f32[2,16,128]{2,1,0:T(8,128)}, u32[]{:S(2)}) copy-start(f32[2,16,128]{2,1,0:T(8,128)} %param.11) | copy-start | bytes 49156
  75.8 33.6 %copy-start.1 = (f32[2,4,1,512]{3,2,1,0:T(1,128)S(1)}, f32[2,4,1,512]{3,2,1,0:T(1,128)}, u32[]{:S(2)}) copy-start(f32[2,4,1,512]{3,2,1,0:T(1,128)} %param.12) | copy-start | bytes 49156
  104.4 3.1 %collective-permute-start = (f32[2,4,1,128]{3,1,0,2:T(4,128)S(1)}, f32[2,4,1,128]{3,1,0,2:T(4,128)S(1)}, u32[]{:S(2)}, u32[]{:S(2)}) collective-permute-start(f32[2,4,1,128]{3,1,0,2:T(4,128)S(1)} %bitcast.115), channel_id=1, source_target_pairs={{0,2},{2,4},{4,6},{6,0},{1,3},{3,5},{5,7},{7,1},{8,10},{10,12},{12... | collective-permute-start | bytes 12296 | tf_op jit(solution)/shard_map/ppermute | solution.py:164
  104.5 3.7 %collective-permute-start.1 = (f32[2,4,1,128]{3,1,0,2:T(4,128)S(1)}, f32[2,4,1,128]{3,1,0,2:T(4,128)S(1)}, u32[]{:S(2)}, u32[]{:S(2)}) collective-permute-start(f32[2,4,1,128]{3,1,0,2:T(4,128)S(1)} %bitcast.114), channel_id=1, source_target_pairs={{0,4},{2,6},{4,0},{6,2},{1,5},{3,7},{5,1},{7,3},{8,12},{10,14},{12... | collective-permute-start | bytes 12296 | tf_op jit(solution)/shard_map/ppermute | solution.py:164
  106.0 2.7 %collective-permute-start.2 = (f32[2,4,1,128]{3,1,0,2:T(4,128)S(1)}, f32[2,4,1,128]{3,1,0,2:T(4,128)S(1)}, u32[]{:S(2)}, u32[]{:S(2)}) collective-permute-start(f32[2,4,1,128]{3,1,0,2:T(4,128)S(1)} %bitcast.113), channel_id=1, source_target_pairs={{0,6},{2,0},{4,2},{6,4},{1,7},{3,1},{5,3},{7,5},{8,14},{10,8},{12,... | collective-permute-start | bytes 12296 | tf_op jit(solution)/shard_map/ppermute | solution.py:164
Sparse Core Ops, SparseCore 0:
  8.9 30.8 all-gather.1
  77.3 14.4 reduce-scatter.1
